TPU v7x, 128 devices: a whole 4x4x4 slice. The times are simulated.
128 devices in a mesh: rows: 16 (over y, z), dp: 8 (over x, core).
Axes of the slice: x: 4, y: 4, z: 4, core: 2. Of those that a mesh axis runs over, the one named last changes fastest.
Arguments:
- weights: float32 [24576, 4096], P(('rows', 'dp'))
- moment: float32 [24576, 4096], P(('rows', 'dp'))
- second: float32 [24576, 4096], P(('rows', 'dp')), may hold values from 0.01 to 1
- tile_rows: bfloat16 [32768, 4096], P(('rows', 'dp')), may hold values from -6 to 6
- row_index: int32 [32768], P(('rows', 'dp')), may hold values from 0 to 191
- bucket_count: int32 [16384], P(('rows', 'dp')), may hold values from 1 to 2, as said below
Outputs:
- new_weights: float32 [24576, 4096], P(('rows', 'dp'))
- new_moment: float32 [24576, 4096], P(('rows', 'dp'))
- new_second: float32 [24576, 4096], P(('rows', 'dp'))
Inputs may be any that keep to these rules, and one draw needn't show every extreme that they name: `bucket_count`: at least one slot of every sender and owner is live; in every draw some owner receives 2 live slots from every sender. `row_index`: rows may repeat within and across senders.
All inputs are finite; a program needn't handle non-finite values.
Results may differ from a plain program's by a relative error of at most 0.0003.
Values may be sent and summed in bfloat16 or wider, within the bound.
No kernel may reach another device: no remote copies, remote signals or barrier semaphores. Data moves between devices by JAX's collectives and lax.ppermute only.
A program may use at most 64 MiB of HBM per device.

v0:
```python
import jax
import jax.numpy as jnp
from jax import lax
from jax.sharding import Mesh
from jax.sharding import PartitionSpec as P

ROWS_DP = ("rows_0", "rows_1", "dp_0", "dp_1")
ROWS = ("rows_0", "rows_1")
DP = ("dp_0", "dp_1")


beta_one = 0.9
beta_two = 0.999
epsilon = 1e-06
decay = 0.01
rate = 0.1


def in_blocks(x, dim, count):
    before, after = (x.shape[:dim], x.shape[dim + 1 :])
    return jnp.moveaxis(x.reshape(*before, count, -1, *after), dim, 0)


def in_order(parts, dim):
    parts = jnp.moveaxis(parts, 0, dim)
    dims = parts.shape
    return parts.reshape(*dims[:dim], dims[dim] * dims[dim + 1], *dims[dim + 2 :])


def joined_exchange(x, axis, axes, splits, concats):
    sizes = [lax.axis_size(a) for a in axes]
    parts = in_blocks(x, splits[0], sizes[0])
    parts = jnp.moveaxis(in_blocks(parts, splits[1] + 1, sizes[1]), 0, 1)
    inside = parts.shape[2:]
    parts = parts.reshape(-1, *inside)
    parts = lax.all_to_all(parts, axis, split_axis=0, concat_axis=0, tiled=True)
    parts = in_order(parts.reshape(*sizes, *inside), concats[0] + 1)
    return in_order(parts, concats[1])


def sent_to_all(x, axis):
    copies = jnp.broadcast_to(x, (lax.axis_size(axis), *x.shape))
    return lax.all_to_all(copies, axis, split_axis=0, concat_axis=0, tiled=True)


def taken_together(x, axis):
    return sent_to_all(x, axis).sum(axis=0)


def by_axis(x, axes):
    far, near = axes
    nearer = taken_together(x, near)
    return taken_together(nearer, far)


def together(arrays, axis):
    ends = [0]
    for a in arrays:
        ends.append(ends[-1] + a.size)
    total = by_axis(jnp.concatenate([a.ravel() for a in arrays]), axis)
    return tuple((total[b:e].reshape(a.shape) for a, b, e in zip(arrays, ends, ends[1:])))


def local(weights, moment, second, tile_rows, row_index, bucket_count):
    owners = lax.axis_size(ROWS_DP)
    rows_here = weights.shape[0]
    slot_total = row_index.shape[0]
    capacity = slot_total // owners
    is_live = lax.broadcasted_iota(jnp.int32, (owners, capacity), 1) < bucket_count[:, None]
    target = jnp.where(is_live.reshape(-1), row_index, -1)
    weight_part = jnp.sum(weights * weights)
    row_groups = lax.axis_size(ROWS)
    replicas = lax.axis_size(DP)
    shaped_rows = tile_rows.reshape(row_groups, replicas, capacity, tile_rows.shape[1])
    shaped_target = target.reshape(row_groups, replicas, capacity)
    got_rows, got_target = (
        joined_exchange(shaped_rows, ROWS_DP, (ROWS, DP), (0, 1), (0, 1)),
        joined_exchange(shaped_target, ROWS_DP, (ROWS, DP), (0, 1), (0, 1)),
    )
    arrived = got_rows.reshape(slot_total, tile_rows.shape[1])
    landing = got_target.reshape(slot_total)
    picker = (
        landing[None, :] == lax.broadcasted_iota(jnp.int32, (rows_here, slot_total), 0)
    ).astype(jnp.bfloat16)
    gradient = jnp.dot(picker, arrived, preferred_element_type=jnp.float32)
    new_moment = beta_one * moment + (1.0 - beta_one) * gradient
    new_second = beta_two * second + (1.0 - beta_two) * gradient * gradient
    update = new_moment / (jnp.sqrt(new_second) + epsilon) + decay * weights
    update_part = jnp.sum(update * update)
    weight_sq, update_sq = together(
        (weight_part, update_part), (("rows_0", "rows_1", "dp_0"), "dp_1")
    )
    trust_ratio = jnp.sqrt(weight_sq) / jnp.sqrt(update_sq + 1e-06)
    new_weights = weights - rate * trust_ratio * update
    return (new_weights, new_moment, new_second)


def solution(mesh):
    torus = Mesh(mesh.devices.reshape(4, 4, 4, 2), ("rows_0", "rows_1", "dp_0", "dp_1"))
    in_specs = (
        P(ROWS_DP, None),
        P(ROWS_DP, None),
        P(ROWS_DP, None),
        P(ROWS_DP, None),
        P(ROWS_DP),
        P(ROWS_DP),
    )
    out_specs = (P(ROWS_DP, None), P(ROWS_DP, None), P(ROWS_DP, None))
    return jax.shard_map(local, mesh=torus, in_specs=in_specs, out_specs=out_specs, check_vma=False)
```

profile of v0, /device:TPU:1, one launch (start us, length us, event | category | flops | bytes accessed | tf_op | source)
XLA Modules:
  0.0 96.6 jit_solution(6065756069724284844)
XLA Ops:
  0.6 0.7 iota_compare_fusion.2
  1.4 0.1 lt.14
  1.5 0.7 broadcast_select_fusion
  2.2 0.8 reshape_transpose_transpose_reshape_reshape_reshape.6
  3.0 11.5 %all-to-all-start = ((s32[128,1,1,2]{3,2,1,0:T(1,128)}), s32[128,1,1,2]{3,2,1,0:T(1,128)S(1)}, u32[]{:S(2)}, u32[]{:S(2)}) async-start(s32[128,1,1,2]{3,2,1,0:T(1,128)} %bitcast.1), calls=%async_computation | async-start | bytes 131072 | tf_op jit(solution)/shard_map/all_to_all | solution.py:36
  14.5 4.4 %reshape_transpose_transpose_reshape_reshape_reshape.7 = bf16[128,1,1,2,4096]{4,3,2,1,0:T(2,128)(2,1)} reshape(bf16[256,4096]{1,0:T(8,128)(2,1)} %param.9) | data formatting | bytes 4194304 | tf_op jit(solution)/shard_map/reshape;transpose;transpose;reshape;reshape;reshape | solution.py:35
  18.9 5.1 %all-to-all-done = s32[128,1,1,2]{3,2,1,0:T(1,128)S(1)} async-done(((s32[128,1,1,2]{3,2,1,0:T(1,128)}), s32[128,1,1,2]{3,2,1,0:T(1,128)S(1)}, u32[]{:S(2)}, u32[]{:S(2)}) %all-to-all-start) | async-done | bytes 1056 | tf_op jit(solution)/shard_map/all_to_all | solution.py:36
  23.9 4.7 %all-to-all-start.1 = ((bf16[128,1,1,2,4096]{4,3,2,1,0:T(2,128)(2,1)}), bf16[128,1,1,2,4096]{4,3,2,1,0:T(2,128)(2,1)S(1)}, u32[]{:S(2)}, u32[]{:S(2)}) async-start(bf16[128,1,1,2,4096]{4,3,2,1,0:T(2,128)(2,1)} %reshape_transpose_transpose_reshape_reshape_reshape.7), calls=%async_computation.1 | async-start | bytes 4194304 | tf_op jit(solution)/shard_map/all_to_all | solution.py:36
  28.6 0.1 eq.10
  28.8 30.3 %all-to-all-done.1 = bf16[128,1,1,2,4096]{4,3,2,1,0:T(2,128)(2,1)S(1)} async-done(((bf16[128,1,1,2,4096]{4,3,2,1,0:T(2,128)(2,1)}), bf16[128,1,1,2,4096]{4,3,2,1,0:T(2,128)(2,1)S(1)}, u32[]{:S(2)}, u32[]{:S(2)}) %all-to-all-start.1) | async-done | bytes 2097184 | tf_op jit(solution)/shard_map/all_to_all | solution.py:36
  59.1 2.2 %reshape_reshape.3 = bf16[256,4096]{1,0:T(8,128)(2,1)} reshape(bf16[16,8,1,2,4096]{4,3,1,0,2:T(2,128)(2,1)S(1)} %bitcast.26) | data formatting | bytes 4194304 | tf_op jit(solution)/shard_map/reshape;reshape | solution.py:80
  61.3 0.0 copy-start
  61.3 8.7 %multiply_reduce_fusion.1 = (f32[]{:T(128)}, f32[]{:T(128)}, f32[192,4096]{1,0:T(8,128)}, f32[192,4096]{1,0:T(8,128)}) fusion(f32[192,4096]{1,0:T(8,128)} %param.6, f32[192,4096]{1,0:T(8,128)} %param.8, f32[192,4096]{1,0:T(8,128)} %param.7, bf16[256,4096]{1,0:T(8,128)(2,1)} %reshape_reshape.3, s32[256]{0:T(256)S(1)} %eq.10), kind=kOutput, calls=%fused_computation.6 | convolution fusion | flops 414498816 | bytes 17826824 | tf_op jit(solution)/shard_map/dot_general | solution.py:85
  70.0 1.3 %pad_maximum_fusion = f32[2]{0:T(128)S(1)} fusion(f32[1]{0:T(128)} %bitcast.10, f32[1]{0:T(128)} %bitcast), kind=kLoop, calls=%fused_computation.11 | loop fusion | flops 2 | bytes 16 | tf_op jit(solution)/shard_map/concatenate | solution.py:60
  71.4 4.3 %all_to_all.22 = f32[2,1,2]{2,1,0:T(1,128)S(1)} all-to-all(f32[2,1,2]{2,1,0:T(1,128)S(1)} %broadcast_in_dim.12), channel_id=1, replica_groups=mesh['rows_0'=4,'rows_1'=4,'dp_0'=4,'dp_1'=2] {'dp_1'}, dimensions={0} | all-to-all | bytes 32 | tf_op jit(solution)/shard_map/all_to_all | solution.py:43
  75.7 12.8 %all_to_all.23 = f32[64,1,2]{2,1,0:T(1,128)S(1)} all-to-all(f32[64,1,2]{2,1,0:T(1,128)S(1)} %broadcast_in_dim.13), channel_id=1, replica_groups=mesh['rows_0'=4,'rows_1'=4,'dp_0'=4,'dp_1'=2] {'rows_0','rows_1','dp_0'}, dimensions={0} | all-to-all | bytes 1024 | tf_op jit(solution)/shard_map/all_to_all | solution.py:43
  88.5 0.1 reduce_sum.39
  88.6 0.6 fusion.4
  90.6 0.0 copy-done
  90.6 5.9 %multiply_subtract_fusion = f32[192,4096]{1,0:T(8,128)} fusion(f32[192,4096]{1,0:T(8,128)S(1)} %copy-done, f32[]{:T(128)} %bitcast.12, f32[192,4096]{1,0:T(8,128)} %get-tuple-element.6, f32[192,4096]{1,0:T(8,128)} %get-tuple-element.5), kind=kLoop, calls=%fused_computation.2 | loop fusion | flops 4718592 | bytes 12582916 | tf_op jit(solution)/shard_map/sub | solution.py:94
  (3 shorter events, 0.0 us)
Async XLA Ops:
  3.0 20.9 %all-to-all-start = ((s32[128,1,1,2]{3,2,1,0:T(1,128)}), s32[128,1,1,2]{3,2,1,0:T(1,128)S(1)}, u32[]{:S(2)}, u32[]{:S(2)}) async-start(s32[128,1,1,2]{3,2,1,0:T(1,128)} %bitcast.1), calls=%async_computation | async-start | bytes 131072 | tf_op jit(solution)/shard_map/all_to_all | solution.py:36
  23.9 35.2 %all-to-all-start.1 = ((bf16[128,1,1,2,4096]{4,3,2,1,0:T(2,128)(2,1)}), bf16[128,1,1,2,4096]{4,3,2,1,0:T(2,128)(2,1)S(1)}, u32[]{:S(2)}, u32[]{:S(2)}) async-start(bf16[128,1,1,2,4096]{4,3,2,1,0:T(2,128)(2,1)} %reshape_transpose_transpose_reshape_reshape_reshape.7), calls=%async_computation.1 | async-start | bytes 4194304 | tf_op jit(solution)/shard_map/all_to_all | solution.py:36
  61.3 29.3 %copy-start = (f32[192,4096]{1,0:T(8,128)S(1)}, f32[192,4096]{1,0:T(8,128)}, u32[]{:S(2)}) copy-start(f32[192,4096]{1,0:T(8,128)} %param.6) | copy-start | bytes 9437188
where the time goes:
time: 97.4 us; the launch traced here: 96.6 us
  waiting for transfers between devices  35.4 us (36%)
  blocking collectives  17.1 us (18%)
  starting transfers between devices  16.2 us (17%)
  other arithmetic  8.79 us (9%)
  matrix products  8.75 us (9%)
  local copies, waits for them, and re-layouts  8.25 us (8%)
  between operations  2.1 us (2%)
    all_to_all x2, waiting for transfers between devices, joined_exchange(): parts = lax.all_to_all(parts, axis, split_axis=0, concat_axis=0, tiled=True)  35.4 us
    all_to_all x2, blocking collectives, sent_to_all(): return lax.all_to_all(copies, axis, split_axis=0, concat_axis=0, tiled=True)  17.1 us
    all_to_all x2, starting transfers between devices, joined_exchange(): parts = lax.all_to_all(parts, axis, split_axis=0, concat_axis=0, tiled=True)  16.2 us
    dot_general x1, matrix products, local(): gradient = jnp.dot(picker, arrived, preferred_element_type=jnp.float32)  8.75 us
    sub x1, other arithmetic, local(): new_weights = weights - rate * trust_ratio * update  5.94 us
    another operation x2, local copies, waits for them, and re-layouts, joined_exchange(): parts = parts.reshape(-1, *inside)  5.16 us
    another operation x1, local copies, waits for them, and re-layouts, local(): arrived = got_rows.reshape(slot_total, tile_rows.shape[1])  2.18 us
  transfers between devices with their start and end apart: 2, of which 2 were waited for; matrix products, arithmetic and copies ran while one was open for 5% of the time, Pallas kernels for 0%

commit v1 on v0

v1 whole, which is shorter than its diff:
```python
import jax
import jax.numpy as jnp
from jax import lax
from jax.experimental import pallas as pl
from jax.experimental.pallas import tpu as pltpu
from jax.sharding import Mesh
from jax.sharding import PartitionSpec as P

AXES = ("rows_0", "rows_1", "dp_0", "dp_1")

beta_one = 0.9
beta_two = 0.999
epsilon = 1e-06
decay = 0.01
rate = 0.1

LANES = 128
VMEM_LIMIT = 20 * 1024 * 1024

any_spec = pl.BlockSpec(memory_space=pl.ANY)
vmem_spec = pl.BlockSpec(memory_space=pltpu.VMEM)
hbm_spec = pl.BlockSpec(memory_space=pltpu.HBM)


def pack_body(rows, index, count, packed, sem):
    owners, capacity, width = packed.shape
    width -= LANES
    slots = owners * capacity
    for b in range(owners):
        pltpu.make_async_copy(
            rows.at[pl.ds(b * capacity, capacity)], packed.at[b, :, pl.ds(0, width)], sem
        ).start()
    at = lax.broadcasted_iota(jnp.int32, (slots, slots), 0)
    spread = jnp.where(at == lax.broadcasted_iota(jnp.int32, (slots, slots), 1), index[...], 0)
    of = lax.broadcasted_iota(jnp.int32, (slots, owners), 0) // capacity
    counts = jnp.where(of == lax.broadcasted_iota(jnp.int32, (slots, owners), 1), count[...], 0)

    def along_lanes(x):
        x = x.astype(jnp.float32).astype(jnp.bfloat16)
        return jnp.dot(x, jnp.ones((x.shape[1], LANES), jnp.bfloat16), preferred_element_type=jnp.float32)

    slot = (lax.broadcasted_iota(jnp.int32, (slots, LANES), 0) % capacity).astype(jnp.float32)
    target = jnp.where(slot < along_lanes(counts), along_lanes(spread), -1.0)
    packed[:, :, pl.ds(width, LANES)] = target.astype(jnp.bfloat16).reshape(owners, capacity, LANES)
    whole = packed.at[:, :, pl.ds(0, width)]
    pltpu.make_async_copy(whole, whole, sem).wait()


def pack(rows, index, count, owners):
    slots, width = rows.shape
    return pl.pallas_call(
        pack_body,
        out_shape=pltpu.VMEM((owners, slots // owners, width + LANES), jnp.bfloat16),
        in_specs=[hbm_spec, vmem_spec, vmem_spec],
        out_specs=vmem_spec,
        scratch_shapes=[pltpu.SemaphoreType.DMA],
        compiler_params=pltpu.CompilerParams(vmem_limit_bytes=VMEM_LIMIT),
        name="pack",
    )(rows, index.reshape(1, slots), count.reshape(1, owners))


CHUNK = 512


def step_body(got, w, m, v, nm_hbm, nv_hbm, u, parts, nm, nv, sems):
    owners, capacity, width = got.shape
    width -= LANES
    slots = owners * capacity
    rows = w.shape[0]
    targets = got[:, :, pl.ds(width, LANES)].reshape(slots, LANES)
    first = (lax.broadcasted_iota(jnp.int32, (8, LANES), 1) == 0).astype(jnp.float32).astype(jnp.bfloat16)
    landing = lax.dot_general(first, targets, (((1,), (1,)), ((), ())), preferred_element_type=jnp.float32)
    row = lax.broadcasted_iota(jnp.int32, (rows, slots), 0).astype(jnp.float32)
    picker = jnp.where(landing[:1, :] == row, 1.0, 0.0).astype(jnp.bfloat16)
    update_sq = jnp.zeros((8, LANES), jnp.float32)
    weight_sq = jnp.zeros((8, LANES), jnp.float32)

    def add_squares(total, x):
        sq = (x * x).reshape(rows // 8, 8, CHUNK).sum(axis=0)
        for i in range(CHUNK // LANES):
            total = total + sq[:, i * LANES : (i + 1) * LANES]
        return total

    for j in range(width // CHUNK):
        at = pl.ds(j * CHUNK, CHUNK)
        arrived = got[:, :, at].reshape(slots, CHUNK)
        g = jnp.dot(picker, arrived, preferred_element_type=jnp.float32)
        new_m = beta_one * m[:, at] + (1.0 - beta_one) * g
        new_v = beta_two * v[:, at] + (1.0 - beta_two) * g * g
        old_w = w[:, at]
        update = new_m / (jnp.sqrt(new_v) + epsilon) + decay * old_w
        nm[:, at] = new_m
        nv[:, at] = new_v
        u[:, at] = update
        for k, (a, b) in enumerate(((nm, nm_hbm), (nv, nv_hbm))):
            pltpu.make_async_copy(a.at[:, at], b.at[:, at], sems.at[k]).start()
        update_sq = add_squares(update_sq, update)
        weight_sq = add_squares(weight_sq, old_w)
    both = jnp.concatenate([x.sum(axis=0, keepdims=True) for x in (update_sq, weight_sq)], axis=1)
    parts[...] = jnp.broadcast_to(both[None], parts.shape)
    for k, (a, b) in enumerate(((nm, nm_hbm), (nv, nv_hbm))):
        pltpu.make_async_copy(a, b, sems.at[k]).wait()


def step(got, w, m, v, peers):
    table = jax.ShapeDtypeStruct(w.shape, jnp.float32)
    return pl.pallas_call(
        step_body,
        out_shape=[table, table, pltpu.VMEM(w.shape, jnp.float32), pltpu.VMEM((peers, 1, 2 * LANES), jnp.float32)],
        in_specs=[vmem_spec] * 4,
        out_specs=[hbm_spec, hbm_spec, vmem_spec, vmem_spec],
        scratch_shapes=[
            pltpu.VMEM(w.shape, jnp.float32),
            pltpu.VMEM(w.shape, jnp.float32),
            pltpu.SemaphoreType.DMA((2,)),
        ],
        compiler_params=pltpu.CompilerParams(vmem_limit_bytes=VMEM_LIMIT),
        name="step",
    )(got, w, m, v)


def finish_body(parts, u, w, out_hbm, out, sem):
    sums = parts[...].reshape(parts.shape[0], parts.shape[2]).sum(axis=0, keepdims=True)
    update_sq = jnp.sum(sums[:, :LANES], axis=1, keepdims=True)
    weight_sq = jnp.sum(sums[:, LANES:], axis=1, keepdims=True)
    scale = rate * (jnp.sqrt(weight_sq) / jnp.sqrt(update_sq + 1e-06))
    for i in range(out.shape[0] // 32):
        at = pl.ds(i * 32, 32)
        out[at, :] = w[at, :] - scale * u[at, :]
        pltpu.make_async_copy(out.at[at, :], out_hbm.at[at, :], sem).start()
    pltpu.make_async_copy(out, out_hbm, sem).wait()


def finish(parts, u, w):
    return pl.pallas_call(
        finish_body,
        out_shape=jax.ShapeDtypeStruct(w.shape, jnp.float32),
        in_specs=[vmem_spec] * 3,
        out_specs=hbm_spec,
        scratch_shapes=[pltpu.VMEM(w.shape, jnp.float32), pltpu.SemaphoreType.DMA],
        compiler_params=pltpu.CompilerParams(vmem_limit_bytes=VMEM_LIMIT),
        name="finish",
    )(parts, u, w)


def local(weights, moment, second, tile_rows, row_index, bucket_count):
    owners = lax.axis_size(AXES)
    tile_rows = pltpu.with_memory_space_constraint(tile_rows, pltpu.HBM)
    w, m, v = (pltpu.with_memory_space_constraint(x, pltpu.VMEM) for x in (weights, moment, second))
    packed = pack(tile_rows, row_index, bucket_count, owners)
    got = lax.all_to_all(packed, AXES, split_axis=0, concat_axis=0, tiled=True)
    new_moment, new_second, update, parts = step(got, w, m, v, owners)
    sums = lax.all_to_all(parts, AXES, split_axis=0, concat_axis=0, tiled=True)
    return (finish(sums, update, w), new_moment, new_second)


def solution(mesh):
    torus = Mesh(mesh.devices.reshape(4, 4, 4, 2), AXES)
    table, flat = P(AXES, None), P(AXES)
    return jax.shard_map(
        local,
        mesh=torus,
        in_specs=(table, table, table, table, flat, flat),
        out_specs=(table, table, table),
        check_vma=False,
    )
```

time: 97.4 us -> 68.3 us (0.70)
  blocking collectives: 17.1 us -> 56.7 us
  waiting for transfers between devices: 35.4 us -> 0 us
  starting transfers between devices: 16.2 us -> 0 us
  other arithmetic: 8.79 us -> 0 us
  matrix products: 8.75 us -> 0 us
  Pallas kernels: 0 us -> 7.47 us
  local copies, waits for them, and re-layouts: 8.25 us -> 3.23 us
  between operations: 2.1 us -> 0.67 us
    all_to_all x2, blocking collectives: 17.1 us -> 56.7 us  [the longest x1 42.5 us: local(): got = lax.all_to_all(packed, AXES, split_axis=0, concat_axis=0, tiled=True)]
    all_to_all x2 -> x0, waiting for transfers between devices: 35.4 us -> none  [joined_exchange(): parts = lax.all_to_all(parts, axis, split_axis=0, concat_axis=0, tiled=True)]
    all_to_all x2 -> x0, starting transfers between devices: 16.2 us -> none  [joined_exchange(): parts = lax.all_to_all(parts, axis, split_axis=0, concat_axis=0, tiled=True)]
    dot_general x1 -> x0, matrix products: 8.75 us -> none  [local(): gradient = jnp.dot(picker, arrived, preferred_element_type=jnp.float32)]
    pallas_call x0 -> x3, Pallas kernels: none -> 7.47 us  [the longest x1 3.88 us: step(): pl.pallas_call(step_body, out_shape=[table, table, pltpu.VMEM(w.shape, jn...]
    another operation x3 -> x0, local copies, waits for them, and re-layouts: 7.34 us -> none  [the longest x2 5.16 us: joined_exchange(): parts = parts.reshape(-1, *inside)]
    sub x1 -> x0, other arithmetic: 5.94 us -> none  [local(): new_weights = weights - rate * trust_ratio * update]
    unnamed x2 -> x10, local copies, waits for them, and re-layouts: 0.01 us -> 3.23 us
  transfers between devices with their start and end apart: 2 -> 0, of which waited for: 2 -> 0; matrix products, arithmetic and copies ran while one was open for 5% -> 0% of each run, Pallas kernels for 0% -> 0%
where the time goes in v1:
time: 68.3 us; the launch traced here: 68.1 us
  blocking collectives  56.7 us (83%)
  Pallas kernels  7.47 us (11%)
  local copies, waits for them, and re-layouts  3.23 us (5%)
    all_to_all x1, blocking collectives, local(): got = lax.all_to_all(packed, AXES, split_axis=0, concat_axis=0, tiled=True)  42.5 us
    all_to_all x1, blocking collectives, local(): sums = lax.all_to_all(parts, AXES, split_axis=0, concat_axis=0, tiled=True)  14.3 us
    pallas_call x1, Pallas kernels, step(): pl.pallas_call(step_body, out_shape=[table, table, pltpu.VMEM(w.shape, jn...  3.88 us
    unnamed x10, local copies, waits for them, and re-layouts  3.23 us
    pallas_call x1, Pallas kernels, finish(): pl.pallas_call(finish_body, out_shape=jax.ShapeDtypeStruct(w.shape, jnp.f...  1.92 us
    pallas_call x1, Pallas kernels, pack(): pl.pallas_call(pack_body, out_shape=pltpu.VMEM((owners, slots // owners,...  1.68 us

profile of v1, /device:TPU:1, one launch (start us, length us, event | category | flops | bytes accessed | tf_op | source)
XLA Modules:
  0.0 68.1 jit_solution(17900419831185493778)
XLA Ops:
  0.6 0.0 copy-start.3
  0.6 0.7 copy-done.3
  1.3 0.0 copy-start.4
  1.3 0.7 copy-done.4
  2.0 0.0 copy-start.1
  2.0 1.7 %pack.1 = bf16[128,2,4224]{2,1,0:T(2,128)(2,1)S(1)} custom-call(bf16[256,4096]{1,0:T(8,128)(2,1)} %rows.1, s32[1,256]{1,0:T(1,128)S(1)} %bitcast.2, s32[1,128]{1,0:T(1,128)S(1)} %bitcast.3), custom_call_target="tpu_custom_call" | custom-call | tf_op jit(solution)/shard_map/pack/pallas_call | solution.py:51
  3.7 0.0 copy-start
  3.7 42.5 %all_to_all.10.got = bf16[128,2,4224]{2,1,0:T(2,128)(2,1)S(1)} all-to-all(bf16[128,2,4224]{2,1,0:T(2,128)(2,1)S(1)} %pack.1), channel_id=1, replica_groups=mesh['rows_0'=4,'rows_1'=4,'dp_0'=4,'dp_1'=2] {'rows_0','rows_1','dp_0',..., dimensions={0} | all-to-all | bytes 4325376 | tf_op jit(solution)/shard_map/all_to_all | solution.py:151
  46.1 0.0 copy-done.1
  46.1 0.0 copy-done
  46.1 0.0 copy-start.2
  46.1 1.9 %copy-done.2 = f32[192,4096]{1,0:T(8,128)S(1)} copy-done((f32[192,4096]{1,0:T(8,128)S(1)}, f32[192,4096]{1,0:T(8,128)}, u32[]{:S(2)}) %copy-start.2) | copy-done | bytes 3145752
  48.0 3.9 %step.1 = (f32[192,4096]{1,0:T(8,128)}, f32[192,4096]{1,0:T(8,128)}, f32[192,4096]{1,0:T(8,128)S(1)}, f32[128,1,256]{2,1,0:T(1,128)S(1)}) custom-call(bf16[128,2,4224]{2,1,0:T(2,128)(2,1)S(1)} %all_to_all.10.got, f32[192,4096]{1,0:T(8,128)S(1)} %copy-done, f32[192,4096]{1,0:T(8,128)S(1)} %copy-done.1, f32[192,4096]{1,0:T(8,128)S(1)} %copy-done.2), custom_call_target="tpu_custom_call" | custom-call | tf_op jit(solution)/shard_map/step/pallas_call | solution.py:107
  51.9 14.3 %all_to_all.11.parts = f32[128,1,256]{2,1,0:T(1,128)S(1)} all-to-all(f32[128,1,256]{2,1,0:T(1,128)S(1)} %get-tuple-element.7), channel_id=1, replica_groups=mesh['rows_0'=4,'rows_1'=4,'dp_0'=4,'dp_1'=2] {'rows_0','rows_1','dp_0',..., dimensions={0} | all-to-all | bytes 262144 | tf_op jit(solution)/shard_map/all_to_all | solution.py:153
  66.2 1.9 %finish.1 = f32[192,4096]{1,0:T(8,128)} custom-call(f32[128,1,256]{2,1,0:T(1,128)S(1)} %all_to_all.11.parts, f32[192,4096]{1,0:T(8,128)S(1)} %get-tuple-element.8.u, f32[192,4096]{1,0:T(8,128)S(1)} %copy-done), custom_call_target="tpu_custom_call" | custom-call | tf_op jit(solution)/shard_map/finish/pallas_call | solution.py:135
Async XLA Ops:
  0.6 0.7 copy-start.3
  1.3 0.7 copy-start.4
  2.0 44.2 %copy-start.1 = (f32[192,4096]{1,0:T(8,128)S(1)}, f32[192,4096]{1,0:T(8,128)}, u32[]{:S(2)}) copy-start(f32[192,4096]{1,0:T(8,128)} %m.1) | copy-start | bytes 9437188
  3.7 42.5 %copy-start = (f32[192,4096]{1,0:T(8,128)S(1)}, f32[192,4096]{1,0:T(8,128)}, u32[]{:S(2)}) copy-start(f32[192,4096]{1,0:T(8,128)} %w.3) | copy-start | bytes 9437188
  46.1 1.9 %copy-start.2 = (f32[192,4096]{1,0:T(8,128)S(1)}, f32[192,4096]{1,0:T(8,128)}, u32[]{:S(2)}) copy-start(f32[192,4096]{1,0:T(8,128)} %v.1) | copy-start | bytes 9437188

commit v2 on v1

--- a/solution.py
+++ b/solution.py
@@ -22,14 +22,30 @@
 hbm_spec = pl.BlockSpec(memory_space=pltpu.HBM)
 
 
-def pack_body(rows, index, count, packed, sem):
+def in_hbm(x):
+    return pltpu.with_memory_space_constraint(x, pltpu.HBM)
+
+
+def in_vmem(x):
+    return pltpu.with_memory_space_constraint(x, pltpu.VMEM)
+
+
+def pack_body(rows, index_hbm, count_hbm, packed, index, count, sem, small):
     owners, capacity, width = packed.shape
     width -= LANES
     slots = owners * capacity
+    short = [
+        pltpu.make_async_copy(a, b, small.at[i])
+        for i, (a, b) in enumerate(((index_hbm, index), (count_hbm, count)))
+    ]
+    for copy in short:
+        copy.start()
     for b in range(owners):
         pltpu.make_async_copy(
             rows.at[pl.ds(b * capacity, capacity)], packed.at[b, :, pl.ds(0, width)], sem
         ).start()
+    for copy in short:
+        copy.wait()
     at = lax.broadcasted_iota(jnp.int32, (slots, slots), 0)
     spread = jnp.where(at == lax.broadcasted_iota(jnp.int32, (slots, slots), 1), index[...], 0)
     of = lax.broadcasted_iota(jnp.int32, (slots, owners), 0) // capacity
@@ -51,22 +67,32 @@
     return pl.pallas_call(
         pack_body,
         out_shape=pltpu.VMEM((owners, slots // owners, width + LANES), jnp.bfloat16),
-        in_specs=[hbm_spec, vmem_spec, vmem_spec],
+        in_specs=[hbm_spec] * 3,
         out_specs=vmem_spec,
-        scratch_shapes=[pltpu.SemaphoreType.DMA],
+        scratch_shapes=[
+            pltpu.VMEM((1, slots), jnp.int32),
+            pltpu.VMEM((1, owners), jnp.int32),
+            pltpu.SemaphoreType.DMA,
+            pltpu.SemaphoreType.DMA((2,)),
+        ],
         compiler_params=pltpu.CompilerParams(vmem_limit_bytes=VMEM_LIMIT),
         name="pack",
-    )(rows, index.reshape(1, slots), count.reshape(1, owners))
+    )(*map(in_hbm, (rows, index.reshape(1, slots), count.reshape(1, owners))))
 
 
 CHUNK = 512
 
 
-def step_body(got, w, m, v, nm_hbm, nv_hbm, u, parts, nm, nv, sems):
+def step_body(got, w, m, v_hbm, nm_hbm, nv_hbm, u, parts, v, nm, nv, sems, v_sems):
     owners, capacity, width = got.shape
     width -= LANES
     slots = owners * capacity
     rows = w.shape[0]
+    fetches = []
+    for j in range(width // CHUNK):
+        at = pl.ds(j * CHUNK, CHUNK)
+        fetches.append(pltpu.make_async_copy(v_hbm.at[:, at], v.at[:, at], v_sems.at[j]))
+        fetches[-1].start()
     targets = got[:, :, pl.ds(width, LANES)].reshape(slots, LANES)
     first = (lax.broadcasted_iota(jnp.int32, (8, LANES), 1) == 0).astype(jnp.float32).astype(jnp.bfloat16)
     landing = lax.dot_general(first, targets, (((1,), (1,)), ((), ())), preferred_element_type=jnp.float32)
@@ -85,6 +111,7 @@
         at = pl.ds(j * CHUNK, CHUNK)
         arrived = got[:, :, at].reshape(slots, CHUNK)
         g = jnp.dot(picker, arrived, preferred_element_type=jnp.float32)
+        fetches[j].wait()
         new_m = beta_one * m[:, at] + (1.0 - beta_one) * g
         new_v = beta_two * v[:, at] + (1.0 - beta_two) * g * g
         old_w = w[:, at]
@@ -107,13 +134,10 @@
     return pl.pallas_call(
         step_body,
         out_shape=[table, table, pltpu.VMEM(w.shape, jnp.float32), pltpu.VMEM((peers, 1, 2 * LANES), jnp.float32)],
-        in_specs=[vmem_spec] * 4,
+        in_specs=[vmem_spec, vmem_spec, vmem_spec, hbm_spec],
         out_specs=[hbm_spec, hbm_spec, vmem_spec, vmem_spec],
-        scratch_shapes=[
-            pltpu.VMEM(w.shape, jnp.float32),
-            pltpu.VMEM(w.shape, jnp.float32),
-            pltpu.SemaphoreType.DMA((2,)),
-        ],
+        scratch_shapes=[pltpu.VMEM(w.shape, jnp.float32)] * 3
+        + [pltpu.SemaphoreType.DMA((2,)), pltpu.SemaphoreType.DMA((w.shape[1] // CHUNK,))],
         compiler_params=pltpu.CompilerParams(vmem_limit_bytes=VMEM_LIMIT),
         name="step",
     )(got, w, m, v)
@@ -145,8 +169,7 @@
 
 def local(weights, moment, second, tile_rows, row_index, bucket_count):
     owners = lax.axis_size(AXES)
-    tile_rows = pltpu.with_memory_space_constraint(tile_rows, pltpu.HBM)
-    w, m, v = (pltpu.with_memory_space_constraint(x, pltpu.VMEM) for x in (weights, moment, second))
+    w, m, v = in_vmem(weights), in_vmem(moment), in_hbm(second)
     packed = pack(tile_rows, row_index, bucket_count, owners)
     got = lax.all_to_all(packed, AXES, split_axis=0, concat_axis=0, tiled=True)
     new_moment, new_second, update, parts = step(got, w, m, v, owners)

time: 68.3 us -> 67.3 us (0.985)
  local copies, waits for them, and re-layouts: 3.23 us -> 0.01 us
  Pallas kernels: 7.47 us -> 9.78 us
    unnamed x10 -> x4, local copies, waits for them, and re-layouts: 3.23 us -> 0.01 us
    pallas_call x1, Pallas kernels: 3.88 us -> 6.01 us  [step(): pl.pallas_call(step_body, out_shape=[table, table, pltpu.VMEM(w.shape, jn...]
where the time goes in v2:
time: 67.3 us; the launch traced here: 67.2 us
  blocking collectives  56.7 us (84%)
  Pallas kernels  9.78 us (15%)
    all_to_all x1, blocking collectives, local(): got = lax.all_to_all(packed, AXES, split_axis=0, concat_axis=0, tiled=True)  42.5 us
    all_to_all x1, blocking collectives, local(): sums = lax.all_to_all(parts, AXES, split_axis=0, concat_axis=0, tiled=True)  14.3 us
    pallas_call x1, Pallas kernels, step(): pl.pallas_call(step_body, out_shape=[table, table, pltpu.VMEM(w.shape, jn...  6.01 us
    pallas_call x1, Pallas kernels, finish(): pl.pallas_call(finish_body, out_shape=jax.ShapeDtypeStruct(w.shape, jnp.f...  1.91 us
    pallas_call x1, Pallas kernels, pack(): pl.pallas_call(pack_body, out_shape=pltpu.VMEM((owners, slots // owners,...  1.86 us

profile of v2, /device:TPU:1, one launch (start us, length us, event | category | flops | bytes accessed | tf_op | source)
XLA Modules:
  0.0 67.2 jit_solution(17578010362029367346)
XLA Ops:
  0.6 0.0 copy-start.1
  0.6 1.9 %pack.1 = bf16[128,2,4224]{2,1,0:T(2,128)(2,1)S(1)} custom-call(bf16[256,4096]{1,0:T(8,128)(2,1)} %rows.1, s32[1,256]{1,0:T(1,128)} %bitcast.2, s32[1,128]{1,0:T(1,128)} %bitcast.3), custom_call_target="tpu_custom_call" | custom-call | tf_op jit(solution)/shard_map/pack/pallas_call | solution.py:67
  2.5 0.0 copy-start
  2.5 42.5 %all_to_all.10.got = bf16[128,2,4224]{2,1,0:T(2,128)(2,1)S(1)} all-to-all(bf16[128,2,4224]{2,1,0:T(2,128)(2,1)S(1)} %pack.1), channel_id=1, replica_groups=mesh['rows_0'=4,'rows_1'=4,'dp_0'=4,'dp_1'=2] {'rows_0','rows_1','dp_0',..., dimensions={0} | all-to-all | bytes 4325376 | tf_op jit(solution)/shard_map/all_to_all | solution.py:174
  45.0 0.0 copy-done.1
  45.0 0.0 copy-done
  45.0 6.0 %step.1 = (f32[192,4096]{1,0:T(8,128)}, f32[192,4096]{1,0:T(8,128)}, f32[192,4096]{1,0:T(8,128)S(1)}, f32[128,1,256]{2,1,0:T(1,128)S(1)}) custom-call(bf16[128,2,4224]{2,1,0:T(2,128)(2,1)S(1)} %all_to_all.10.got, f32[192,4096]{1,0:T(8,128)S(1)} %copy-done, f32[192,4096]{1,0:T(8,128)S(1)} %copy-done.1, f32[192,4096]{1,0:T(8,128)} %v_hbm.1), custom_call_target="tpu_custom_call" | custom-call | tf_op jit(solution)/shard_map/step/pallas_call | solution.py:134
  51.0 14.3 %all_to_all.11.parts = f32[128,1,256]{2,1,0:T(1,128)S(1)} all-to-all(f32[128,1,256]{2,1,0:T(1,128)S(1)} %get-tuple-element.7), channel_id=1, replica_groups=mesh['rows_0'=4,'rows_1'=4,'dp_0'=4,'dp_1'=2] {'rows_0','rows_1','dp_0',..., dimensions={0} | all-to-all | bytes 262144 | tf_op jit(solution)/shard_map/all_to_all | solution.py:176
  65.3 1.9 %finish.1 = f32[192,4096]{1,0:T(8,128)} custom-call(f32[128,1,256]{2,1,0:T(1,128)S(1)} %all_to_all.11.parts, f32[192,4096]{1,0:T(8,128)S(1)} %get-tuple-element.8.u, f32[192,4096]{1,0:T(8,128)S(1)} %copy-done), custom_call_target="tpu_custom_call" | custom-call | tf_op jit(solution)/shard_map/finish/pallas_call | solution.py:159
Async XLA Ops:
  0.6 44.3 %copy-start.1 = (f32[192,4096]{1,0:T(8,128)S(1)}, f32[192,4096]{1,0:T(8,128)}, u32[]{:S(2)}) copy-start(f32[192,4096]{1,0:T(8,128)} %m.1) | copy-start | bytes 9437188
  2.5 42.5 %copy-start = (f32[192,4096]{1,0:T(8,128)S(1)}, f32[192,4096]{1,0:T(8,128)}, u32[]{:S(2)}) copy-start(f32[192,4096]{1,0:T(8,128)} %w.3) | copy-start | bytes 9437188

commit v3 on v2

--- a/solution.py
+++ b/solution.py
@@ -81,18 +81,28 @@
 
 
 CHUNK = 512
-
-
-def step_body(got, w, m, v_hbm, nm_hbm, nv_hbm, u, parts, v, nm, nv, sems, v_sems):
+AHEAD = 2
+
+
+def chunks(width):
+    starts = list(range(0, width - CHUNK, CHUNK))
+    spans = [(at, CHUNK) for at in starts]
+    return spans + [(width - CHUNK, CHUNK // 2), (width - CHUNK // 2, CHUNK // 2)]
+
+
+def step_body(got, w, m, v_hbm, nm_hbm, nv_hbm, u, parts, v, nm, nv, grad, sems, v_sems):
     owners, capacity, width = got.shape
     width -= LANES
     slots = owners * capacity
     rows = w.shape[0]
-    fetches = []
-    for j in range(width // CHUNK):
-        at = pl.ds(j * CHUNK, CHUNK)
-        fetches.append(pltpu.make_async_copy(v_hbm.at[:, at], v.at[:, at], v_sems.at[j]))
-        fetches[-1].start()
+    spans = chunks(width)
+
+    def fetch(j):
+        at = pl.ds(*spans[j])
+        return pltpu.make_async_copy(v_hbm.at[:, at], v.at[:, at], v_sems.at[j])
+
+    for j in range(AHEAD):
+        fetch(j).start()
     targets = got[:, :, pl.ds(width, LANES)].reshape(slots, LANES)
     first = (lax.broadcasted_iota(jnp.int32, (8, LANES), 1) == 0).astype(jnp.float32).astype(jnp.bfloat16)
     landing = lax.dot_general(first, targets, (((1,), (1,)), ((), ())), preferred_element_type=jnp.float32)
@@ -100,29 +110,30 @@
     picker = jnp.where(landing[:1, :] == row, 1.0, 0.0).astype(jnp.bfloat16)
     update_sq = jnp.zeros((8, LANES), jnp.float32)
     weight_sq = jnp.zeros((8, LANES), jnp.float32)
-
-    def add_squares(total, x):
-        sq = (x * x).reshape(rows // 8, 8, CHUNK).sum(axis=0)
-        for i in range(CHUNK // LANES):
-            total = total + sq[:, i * LANES : (i + 1) * LANES]
-        return total
-
-    for j in range(width // CHUNK):
-        at = pl.ds(j * CHUNK, CHUNK)
-        arrived = got[:, :, at].reshape(slots, CHUNK)
-        g = jnp.dot(picker, arrived, preferred_element_type=jnp.float32)
-        fetches[j].wait()
-        new_m = beta_one * m[:, at] + (1.0 - beta_one) * g
-        new_v = beta_two * v[:, at] + (1.0 - beta_two) * g * g
-        old_w = w[:, at]
-        update = new_m / (jnp.sqrt(new_v) + epsilon) + decay * old_w
-        nm[:, at] = new_m
-        nv[:, at] = new_v
-        u[:, at] = update
+    for j, (start, size) in enumerate(spans):
+        at = pl.ds(start, size)
+        if j + AHEAD < len(spans):
+            fetch(j + AHEAD).start()
+        arrived = got[:, :, at].reshape(slots, size)
+        grad[j % 2, :, pl.ds(0, size)] = jnp.dot(picker, arrived, preferred_element_type=jnp.float32)
+        fetch(j).wait()
+        for r in range(0, rows, 8):
+            here = (pl.ds(r, 8), at)
+            g = grad[j % 2, pl.ds(r, 8), pl.ds(0, size)]
+            old_w = w[here]
+            new_m = beta_one * m[here] + (1.0 - beta_one) * g
+            new_v = beta_two * v[here] + (1.0 - beta_two) * g * g
+            update = new_m / (new_v * lax.rsqrt(new_v) + epsilon) + decay * old_w
+            nm[here] = new_m
+            nv[here] = new_v
+            u[here] = update
+            for i in range(0, size, LANES):
+                part = update[:, i : i + LANES]
+                update_sq = update_sq + part * part
+                part = old_w[:, i : i + LANES]
+                weight_sq = weight_sq + part * part
         for k, (a, b) in enumerate(((nm, nm_hbm), (nv, nv_hbm))):
             pltpu.make_async_copy(a.at[:, at], b.at[:, at], sems.at[k]).start()
-        update_sq = add_squares(update_sq, update)
-        weight_sq = add_squares(weight_sq, old_w)
     both = jnp.concatenate([x.sum(axis=0, keepdims=True) for x in (update_sq, weight_sq)], axis=1)
     parts[...] = jnp.broadcast_to(both[None], parts.shape)
     for k, (a, b) in enumerate(((nm, nm_hbm), (nv, nv_hbm))):
@@ -137,7 +148,11 @@
         in_specs=[vmem_spec, vmem_spec, vmem_spec, hbm_spec],
         out_specs=[hbm_spec, hbm_spec, vmem_spec, vmem_spec],
         scratch_shapes=[pltpu.VMEM(w.shape, jnp.float32)] * 3
-        + [pltpu.SemaphoreType.DMA((2,)), pltpu.SemaphoreType.DMA((w.shape[1] // CHUNK,))],
+        + [
+            pltpu.VMEM((2, w.shape[0], CHUNK), jnp.float32),
+            pltpu.SemaphoreType.DMA((2,)),
+            pltpu.SemaphoreType.DMA((len(chunks(w.shape[1])),)),
+        ],
         compiler_params=pltpu.CompilerParams(vmem_limit_bytes=VMEM_LIMIT),
         name="step",
     )(got, w, m, v)

time: 67.3 us -> 66.8 us (level)
  no operation moved by 1% of the time
where the time goes in v3:
time: 66.8 us; the launch traced here: 66.6 us
  blocking collectives  56.7 us (85%)
  Pallas kernels  9.21 us (14%)
  between operations  0.67 us (1%)
    all_to_all x1, blocking collectives, local(): got = lax.all_to_all(packed, AXES, split_axis=0, concat_axis=0, tiled=True)  42.5 us
    all_to_all x1, blocking collectives, local(): sums = lax.all_to_all(parts, AXES, split_axis=0, concat_axis=0, tiled=True)  14.3 us
    pallas_call x1, Pallas kernels, step(): pl.pallas_call(step_body, out_shape=[table, table, pltpu.VMEM(w.shape, jn...  5.44 us
    pallas_call x1, Pallas kernels, finish(): pl.pallas_call(finish_body, out_shape=jax.ShapeDtypeStruct(w.shape, jnp.f...  1.91 us
    pallas_call x1, Pallas kernels, pack(): pl.pallas_call(pack_body, out_shape=pltpu.VMEM((owners, slots // owners,...  1.86 us

profile of v3, /device:TPU:1, one launch (start us, length us, event | category | flops | bytes accessed | tf_op | source)
XLA Modules:
  0.0 66.6 jit_solution(7869548990624324159)
XLA Ops:
  0.6 0.0 copy-start.1
  0.6 1.9 %pack.1 = bf16[128,2,4224]{2,1,0:T(2,128)(2,1)S(1)} custom-call(bf16[256,4096]{1,0:T(8,128)(2,1)} %rows.1, s32[1,256]{1,0:T(1,128)} %bitcast.2, s32[1,128]{1,0:T(1,128)} %bitcast.3), custom_call_target="tpu_custom_call" | custom-call | tf_op jit(solution)/shard_map/pack/pallas_call | solution.py:67
  2.5 0.0 copy-start
  2.5 42.5 %all_to_all.10.got = bf16[128,2,4224]{2,1,0:T(2,128)(2,1)S(1)} all-to-all(bf16[128,2,4224]{2,1,0:T(2,128)(2,1)S(1)} %pack.1), channel_id=1, replica_groups=mesh['rows_0'=4,'rows_1'=4,'dp_0'=4,'dp_1'=2] {'rows_0','rows_1','dp_0',..., dimensions={0} | all-to-all | bytes 4325376 | tf_op jit(solution)/shard_map/all_to_all | solution.py:189
  45.0 0.0 copy-done.1
  45.0 0.0 copy-done
  45.0 5.4 %step.1 = (f32[192,4096]{1,0:T(8,128)}, f32[192,4096]{1,0:T(8,128)}, f32[192,4096]{1,0:T(8,128)S(1)}, f32[128,1,256]{2,1,0:T(1,128)S(1)}) custom-call(bf16[128,2,4224]{2,1,0:T(2,128)(2,1)S(1)} %all_to_all.10.got, f32[192,4096]{1,0:T(8,128)S(1)} %copy-done, f32[192,4096]{1,0:T(8,128)S(1)} %copy-done.1, f32[192,4096]{1,0:T(8,128)} %v_hbm.1), custom_call_target="tpu_custom_call" | custom-call | tf_op jit(solution)/shard_map/step/pallas_call | solution.py:145
  50.4 14.3 %all_to_all.11.parts = f32[128,1,256]{2,1,0:T(1,128)S(1)} all-to-all(f32[128,1,256]{2,1,0:T(1,128)S(1)} %get-tuple-element.7), channel_id=1, replica_groups=mesh['rows_0'=4,'rows_1'=4,'dp_0'=4,'dp_1'=2] {'rows_0','rows_1','dp_0',..., dimensions={0} | all-to-all | bytes 262144 | tf_op jit(solution)/shard_map/all_to_all | solution.py:191
  64.7 1.9 %finish.1 = f32[192,4096]{1,0:T(8,128)} custom-call(f32[128,1,256]{2,1,0:T(1,128)S(1)} %all_to_all.11.parts, f32[192,4096]{1,0:T(8,128)S(1)} %get-tuple-element.8.u, f32[192,4096]{1,0:T(8,128)S(1)} %copy-done), custom_call_target="tpu_custom_call" | custom-call | tf_op jit(solution)/shard_map/finish/pallas_call | solution.py:174
Async XLA Ops:
  0.6 44.3 %copy-start.1 = (f32[192,4096]{1,0:T(8,128)S(1)}, f32[192,4096]{1,0:T(8,128)}, u32[]{:S(2)}) copy-start(f32[192,4096]{1,0:T(8,128)} %m.1) | copy-start | bytes 9437188
  2.5 42.5 %copy-start = (f32[192,4096]{1,0:T(8,128)S(1)}, f32[192,4096]{1,0:T(8,128)}, u32[]{:S(2)}) copy-start(f32[192,4096]{1,0:T(8,128)} %w.3) | copy-start | bytes 9437188

commit v4 on v2

v4 whole, which is shorter than its diff:
```python
import jax
import jax.numpy as jnp
from jax import lax
from jax.experimental import pallas as pl
from jax.experimental.pallas import tpu as pltpu
from jax.sharding import Mesh
from jax.sharding import PartitionSpec as P

AXES = ("rows_0", "rows_1", "dp_0", "dp_1")

beta_one = 0.9
beta_two = 0.999
epsilon = 1e-06
decay = 0.01
rate = 0.1

LANES = 128
PACK_FLOPS = 4_000_000_000
VMEM_LIMIT = 20 * 1024 * 1024

any_spec = pl.BlockSpec(memory_space=pl.ANY)
vmem_spec = pl.BlockSpec(memory_space=pltpu.VMEM)
hbm_spec = pl.BlockSpec(memory_space=pltpu.HBM)


def in_hbm(x):
    return pltpu.with_memory_space_constraint(x, pltpu.HBM)


def in_vmem(x):
    return pltpu.with_memory_space_constraint(x, pltpu.VMEM)


def pack_body(rows, index_hbm, count_hbm, packed, index, count, sem, small):
    owners, capacity, width = packed.shape
    width -= LANES
    slots = owners * capacity
    short = [
        pltpu.make_async_copy(a, b, small.at[i])
        for i, (a, b) in enumerate(((index_hbm, index), (count_hbm, count)))
    ]
    for copy in short:
        copy.start()
    for b in range(owners):
        pltpu.make_async_copy(
            rows.at[pl.ds(b * capacity, capacity)], packed.at[b, :, pl.ds(0, width)], sem
        ).start()
    for copy in short:
        copy.wait()
    at = lax.broadcasted_iota(jnp.int32, (slots, slots), 0)
    spread = jnp.where(at == lax.broadcasted_iota(jnp.int32, (slots, slots), 1), index[...], 0)
    of = lax.broadcasted_iota(jnp.int32, (slots, owners), 0) // capacity
    counts = jnp.where(of == lax.broadcasted_iota(jnp.int32, (slots, owners), 1), count[...], 0)

    def along_lanes(x):
        x = x.astype(jnp.float32).astype(jnp.bfloat16)
        return jnp.dot(x, jnp.ones((x.shape[1], LANES), jnp.bfloat16), preferred_element_type=jnp.float32)

    slot = (lax.broadcasted_iota(jnp.int32, (slots, LANES), 0) % capacity).astype(jnp.float32)
    target = jnp.where(slot < along_lanes(counts), along_lanes(spread), -1.0)
    packed[:, :, pl.ds(width, LANES)] = target.astype(jnp.bfloat16).reshape(owners, capacity, LANES)
    whole = packed.at[:, :, pl.ds(0, width)]
    pltpu.make_async_copy(whole, whole, sem).wait()


def pack(rows, index, count, owners):
    slots, width = rows.shape
    return pl.pallas_call(
        pack_body,
        out_shape=pltpu.VMEM((owners, slots // owners, width + LANES), jnp.bfloat16),
        in_specs=[hbm_spec] * 3,
        out_specs=vmem_spec,
        scratch_shapes=[
            pltpu.VMEM((1, slots), jnp.int32),
            pltpu.VMEM((1, owners), jnp.int32),
            pltpu.SemaphoreType.DMA,
            pltpu.SemaphoreType.DMA((2,)),
        ],
        compiler_params=pltpu.CompilerParams(vmem_limit_bytes=VMEM_LIMIT),
        cost_estimate=pl.CostEstimate(flops=PACK_FLOPS, transcendentals=0, bytes_accessed=0),
        name="pack",
    )(*map(in_hbm, (rows, index.reshape(1, slots), count.reshape(1, owners))))


CHUNK = 512
LATE = 2 * CHUNK


def step_body(got, w, m, v, nm_hbm, nv_hbm, u, parts, late_m, late_v, nm, nv, grad, sems):
    owners, capacity, width = got.shape
    width -= LANES
    slots = owners * capacity
    rows = w.shape[0]
    early = width - LATE

    def gradient(j):
        arrived = got[:, :, pl.ds(j * CHUNK, CHUNK)].reshape(slots, CHUNK)
        grad[j % 2] = jnp.dot(picker, arrived, preferred_element_type=jnp.float32)

    targets = got[:, :, pl.ds(width, LANES)].reshape(slots, LANES)
    first = (lax.broadcasted_iota(jnp.int32, (8, LANES), 1) == 0).astype(jnp.float32).astype(jnp.bfloat16)
    landing = lax.dot_general(first, targets, (((1,), (1,)), ((), ())), preferred_element_type=jnp.float32)
    row = lax.broadcasted_iota(jnp.int32, (rows, slots), 0).astype(jnp.float32)
    picker = jnp.where(landing[:1, :] == row, 1.0, 0.0).astype(jnp.bfloat16)
    gradient(0)

    def add_squares(total, x):
        for i in range(0, x.shape[1], LANES):
            part = x[:, i : i + LANES]
            total = total + part * part
        return total

    weight_sq = [jnp.zeros((8, LANES), jnp.float32)] * 4
    for r in range(0, rows, 8):
        for i in range(4):
            weight_sq[i] = add_squares(weight_sq[i], w[pl.ds(r, 8), pl.ds(i * (width // 4), width // 4)])
    weight_sq = (weight_sq[0] + weight_sq[1]) + (weight_sq[2] + weight_sq[3])
    update_sq = [jnp.zeros((8, LANES), jnp.float32)] * 2
    for j in range(width // CHUNK):
        at = pl.ds(j * CHUNK, CHUNK)
        if j:
            gradient(j)
        is_early = j * CHUNK < early
        to_m, to_v = (nm, nv) if is_early else (late_m, late_v)
        to = at if is_early else pl.ds(j * CHUNK - early, CHUNK)
        for r in range(0, rows, 8):
            tile = pl.ds(r, 8)
            g = grad[j % 2, tile, :]
            new_m = beta_one * m[tile, at] + (1.0 - beta_one) * g
            new_v = beta_two * v[tile, at] + (1.0 - beta_two) * g * g
            update = new_m / (new_v * lax.rsqrt(new_v) + epsilon) + decay * w[tile, at]
            to_m[tile, to] = new_m
            to_v[tile, to] = new_v
            u[tile, at] = update
            update_sq[r // 8 % 2] = add_squares(update_sq[r // 8 % 2], update)
        if is_early:
            for k, (a, b) in enumerate(((nm, nm_hbm), (nv, nv_hbm))):
                pltpu.make_async_copy(a.at[:, at], b.at[:, at], sems.at[k]).start()
    sums = [x.sum(axis=0, keepdims=True) for x in (update_sq[0] + update_sq[1], weight_sq)]
    parts[...] = jnp.broadcast_to(jnp.concatenate(sums, axis=1)[None], parts.shape)
    for k, (a, b) in enumerate(((nm, nm_hbm), (nv, nv_hbm))):
        pltpu.make_async_copy(a, b.at[:, pl.ds(0, early)], sems.at[k]).wait()


def step(got, w, m, v, peers):
    rows, width = w.shape
    table = jax.ShapeDtypeStruct(w.shape, jnp.float32)
    late = pltpu.VMEM((rows, LATE), jnp.float32)
    return pl.pallas_call(
        step_body,
        out_shape=[table, table, pltpu.VMEM(w.shape, jnp.float32), pltpu.VMEM((peers, 1, 2 * LANES), jnp.float32), late, late],
        in_specs=[vmem_spec] * 4,
        out_specs=[hbm_spec, hbm_spec] + [vmem_spec] * 4,
        scratch_shapes=[
            pltpu.VMEM((rows, width - LATE), jnp.float32),
            pltpu.VMEM((rows, width - LATE), jnp.float32),
            pltpu.VMEM((2, rows, CHUNK), jnp.float32),
            pltpu.SemaphoreType.DMA((2,)),
        ],
        compiler_params=pltpu.CompilerParams(vmem_limit_bytes=VMEM_LIMIT),
        name="step",
    )(got, w, m, v)


def finish_body(parts, u, w, late_m, late_v, nm_in, nv_in, out_hbm, nm_hbm, nv_hbm, out, sem, late_sems):
    columns = pl.ds(nm_hbm.shape[1] - late_m.shape[1], late_m.shape[1])
    late = [
        pltpu.make_async_copy(a, b.at[:, columns], late_sems.at[i])
        for i, (a, b) in enumerate(((late_m, nm_hbm), (late_v, nv_hbm)))
    ]
    for copy in late:
        copy.start()
    sums = parts[...].reshape(parts.shape[0], parts.shape[2]).sum(axis=0, keepdims=True)
    update_sq = jnp.sum(sums[:, :LANES], axis=1, keepdims=True)
    weight_sq = jnp.sum(sums[:, LANES:], axis=1, keepdims=True)
    scale = rate * (jnp.sqrt(weight_sq) / jnp.sqrt(update_sq + 1e-06))
    block = 16
    for i in range(0, out.shape[0], block):
        for r in range(i, i + block, 8):
            tile = pl.ds(r, 8)
            out[tile, :] = w[tile, :] - scale * u[tile, :]
        at = pl.ds(i, block)
        pltpu.make_async_copy(out.at[at, :], out_hbm.at[at, :], sem).start()
    for copy in late:
        copy.wait()
    pltpu.make_async_copy(out, out_hbm, sem).wait()


def finish(parts, u, w, late_m, late_v, new_moment, new_second):
    table = jax.ShapeDtypeStruct(w.shape, jnp.float32)
    return pl.pallas_call(
        finish_body,
        out_shape=[table] * 3,
        in_specs=[vmem_spec] * 5 + [hbm_spec] * 2,
        out_specs=[hbm_spec] * 3,
        input_output_aliases={5: 1, 6: 2},
        scratch_shapes=[
            pltpu.VMEM(w.shape, jnp.float32),
            pltpu.SemaphoreType.DMA,
            pltpu.SemaphoreType.DMA((2,)),
        ],
        compiler_params=pltpu.CompilerParams(vmem_limit_bytes=VMEM_LIMIT),
        name="finish",
    )(parts, u, w, late_m, late_v, new_moment, new_second)


def local(weights, moment, second, tile_rows, row_index, bucket_count):
    owners = lax.axis_size(AXES)
    w, m, v = in_vmem(weights), in_vmem(moment), in_vmem(second)
    packed = pack(tile_rows, row_index, bucket_count, owners)
    got = lax.all_to_all(packed, AXES, split_axis=0, concat_axis=0, tiled=True)
    new_moment, new_second, update, parts, late_m, late_v = step(got, w, m, v, owners)
    sums = lax.all_to_all(parts, AXES, split_axis=0, concat_axis=0, tiled=True)
    return tuple(finish(sums, update, w, late_m, late_v, new_moment, new_second))


def solution(mesh):
    torus = Mesh(mesh.devices.reshape(4, 4, 4, 2), AXES)
    table, flat = P(AXES, None), P(AXES)
    return jax.shard_map(
        local,
        mesh=torus,
        in_specs=(table, table, table, table, flat, flat),
        out_specs=(table, table, table),
        check_vma=False,
    )
```

time: 67.3 us -> 64.6 us (0.960)
  Pallas kernels: 9.78 us -> 7.04 us
    pallas_call x1, Pallas kernels: 6.01 us -> 2.81 us  [step(): pl.pallas_call(step_body, out_shape=[table, table, pltpu.VMEM(w.shape, jn...]
where the time goes in v4:
time: 64.6 us; the launch traced here: 64.5 us
  blocking collectives  56.7 us (88%)
  Pallas kernels  7.04 us (11%)
  between operations  0.68 us (1%)
    all_to_all x1, blocking collectives, local(): got = lax.all_to_all(packed, AXES, split_axis=0, concat_axis=0, tiled=True)  42.5 us
    all_to_all x1, blocking collectives, local(): sums = lax.all_to_all(parts, AXES, split_axis=0, concat_axis=0, tiled=True)  14.3 us
    pallas_call x1, Pallas kernels, step(): pl.pallas_call(step_body, out_shape=[table, table, pltpu.VMEM(w.shape, jn...  2.81 us
    pallas_call x1, Pallas kernels, finish(): pl.pallas_call(finish_body, out_shape=[table] * 3, in_specs=[vmem_spec] *...  2.38 us
    pallas_call x1, Pallas kernels, pack(): pl.pallas_call(pack_body, out_shape=pltpu.VMEM((owners, slots // owners,...  1.85 us

profile of v4, /device:TPU:1, one launch (start us, length us, event | category | flops | bytes accessed | tf_op | source)
XLA Modules:
  0.0 64.5 jit_solution(15177146764542199182)
XLA Ops:
  0.6 0.0 copy-start.1
  0.6 0.0 copy-start.2
  0.7 1.8 %pack.1 = bf16[128,2,4224]{2,1,0:T(2,128)(2,1)S(1)} custom-call(bf16[256,4096]{1,0:T(8,128)(2,1)} %rows.1, s32[1,256]{1,0:T(1,128)} %bitcast.2, s32[1,128]{1,0:T(1,128)} %bitcast.3), custom_call_target="tpu_custom_call" | custom-call | flops 4000000000 | tf_op jit(solution)/shard_map/pack/pallas_call | solution.py:68
  2.5 0.0 copy-start
  2.5 42.5 %all_to_all.10.got = bf16[128,2,4224]{2,1,0:T(2,128)(2,1)S(1)} all-to-all(bf16[128,2,4224]{2,1,0:T(2,128)(2,1)S(1)} %pack.1), channel_id=1, replica_groups=mesh['rows_0'=4,'rows_1'=4,'dp_0'=4,'dp_1'=2] {'rows_0','rows_1','dp_0',..., dimensions={0} | all-to-all | bytes 4325376 | tf_op jit(solution)/shard_map/all_to_all | solution.py:211
  45.0 0.0 copy-done.1
  45.0 0.0 copy-done.2
  45.0 0.0 copy-done
  45.0 2.8 %step.1 = (f32[192,4096]{1,0:T(8,128)}, f32[192,4096]{1,0:T(8,128)}, f32[192,4096]{1,0:T(8,128)S(1)}, f32[128,1,256]{2,1,0:T(1,128)S(1)}, f32[192,1024]{1,0:T(8,128)S(1)}, /*index=5*/f32[192,1024]{1,0:T(8,128)S(1)}) custom-call(bf16[128,2,4224]{2,1,0:T(2,128)(2,1)S(1)} %all_to_all.10.got, f32[192,4096]{1,0:T(8,128)S(1)} %copy-done, ...), custom_call_target="tpu_custom_call" | custom-call | tf_op jit(solution)/shard_map/step/pallas_call | solution.py:149
  47.8 14.3 %all_to_all.11.parts = f32[128,1,256]{2,1,0:T(1,128)S(1)} all-to-all(f32[128,1,256]{2,1,0:T(1,128)S(1)} %get-tuple-element.9), channel_id=1, replica_groups=mesh['rows_0'=4,'rows_1'=4,'dp_0'=4,'dp_1'=2] {'rows_0','rows_1','dp_0',..., dimensions={0} | all-to-all | bytes 262144 | tf_op jit(solution)/shard_map/all_to_all | solution.py:213
  62.1 2.4 %finish.1 = (f32[192,4096]{1,0:T(8,128)}, f32[192,4096]{1,0:T(8,128)}, f32[192,4096]{1,0:T(8,128)}) custom-call(f32[128,1,256]{2,1,0:T(1,128)S(1)} %all_to_all.11.parts, f32[192,4096]{1,0:T(8,128)S(1)} %get-tuple-element.10.u, f32[192,4096]{1,0:T(8,128)S(1)} %copy-done, ...), custom_call_target="tpu_custom_call", output_to_operand_aliasing={{1}: (5, {}), {2}: (6, {})} | custom-call | tf_op jit(solution)/shard_map/finish/pallas_call | solution.py:191
Async XLA Ops:
  0.6 44.3 %copy-start.1 = (f32[192,4096]{1,0:T(8,128)S(1)}, f32[192,4096]{1,0:T(8,128)}, u32[]{:S(2)}) copy-start(f32[192,4096]{1,0:T(8,128)} %m.1) | copy-start | bytes 9437188
  0.6 44.3 %copy-start.2 = (f32[192,4096]{1,0:T(8,128)S(1)}, f32[192,4096]{1,0:T(8,128)}, u32[]{:S(2)}) copy-start(f32[192,4096]{1,0:T(8,128)} %v.1) | copy-start | bytes 9437188
  2.5 42.5 %copy-start = (f32[192,4096]{1,0:T(8,128)S(1)}, f32[192,4096]{1,0:T(8,128)}, u32[]{:S(2)}) copy-start(f32[192,4096]{1,0:T(8,128)} %w.3) | copy-start | bytes 9437188

commit v5 on v4

--- a/solution.py
+++ b/solution.py
@@ -1,3 +1,5 @@
+import functools
+
 import jax
 import jax.numpy as jnp
 from jax import lax
@@ -7,6 +9,7 @@
 from jax.sharding import PartitionSpec as P
 
 AXES = ("rows_0", "rows_1", "dp_0", "dp_1")
+TURN = (2, 3, 0, 1)
 
 beta_one = 0.9
 beta_two = 0.999
@@ -31,7 +34,18 @@
     return pltpu.with_memory_space_constraint(x, pltpu.VMEM)
 
 
-def pack_body(rows, index_hbm, count_hbm, packed, index, count, sem, small):
+def owner_at(place, sizes):
+    parts = [None] * len(sizes)
+    for axis in reversed(TURN):
+        parts[axis] = place & (sizes[axis] - 1)
+        place = place >> (sizes[axis].bit_length() - 1)
+    owner = 0
+    for part, size in zip(parts, sizes):
+        owner = owner * size + part
+    return owner
+
+
+def pack_body(sizes, rows, index_hbm, count_hbm, packed, index, count, sem, small):
     owners, capacity, width = packed.shape
     width -= LANES
     slots = owners * capacity
@@ -43,21 +57,29 @@
         copy.start()
     for b in range(owners):
         pltpu.make_async_copy(
-            rows.at[pl.ds(b * capacity, capacity)], packed.at[b, :, pl.ds(0, width)], sem
+            rows.at[pl.ds(owner_at(b, sizes) * capacity, capacity)], packed.at[b, :, pl.ds(0, width)], sem
         ).start()
     for copy in short:
         copy.wait()
-    at = lax.broadcasted_iota(jnp.int32, (slots, slots), 0)
-    spread = jnp.where(at == lax.broadcasted_iota(jnp.int32, (slots, slots), 1), index[...], 0)
-    of = lax.broadcasted_iota(jnp.int32, (slots, owners), 0) // capacity
-    counts = jnp.where(of == lax.broadcasted_iota(jnp.int32, (slots, owners), 1), count[...], 0)
+    def slot_at(shape):
+        at = lax.broadcasted_iota(jnp.int32, shape, 0)
+        low = capacity.bit_length() - 1
+        return (owner_at(at >> low, sizes) << low) + (at & (capacity - 1))
+
+    at = slot_at((slots, owners))
+    lane = lax.broadcasted_iota(jnp.int32, (slots, owners), 1)
+    spread = [
+        jnp.where(at == lane + i, index[:, pl.ds(i, owners)], 0) for i in range(0, slots, owners)
+    ]
+    of = at >> (capacity.bit_length() - 1)
+    counts = jnp.where(of == lane, count[...], 0)
 
     def along_lanes(x):
         x = x.astype(jnp.float32).astype(jnp.bfloat16)
         return jnp.dot(x, jnp.ones((x.shape[1], LANES), jnp.bfloat16), preferred_element_type=jnp.float32)
 
     slot = (lax.broadcasted_iota(jnp.int32, (slots, LANES), 0) % capacity).astype(jnp.float32)
-    target = jnp.where(slot < along_lanes(counts), along_lanes(spread), -1.0)
+    target = jnp.where(slot < along_lanes(counts), sum(along_lanes(x) for x in spread), -1.0)
     packed[:, :, pl.ds(width, LANES)] = target.astype(jnp.bfloat16).reshape(owners, capacity, LANES)
     whole = packed.at[:, :, pl.ds(0, width)]
     pltpu.make_async_copy(whole, whole, sem).wait()
@@ -66,7 +88,7 @@
 def pack(rows, index, count, owners):
     slots, width = rows.shape
     return pl.pallas_call(
-        pack_body,
+        functools.partial(pack_body, tuple(lax.axis_size(a) for a in AXES)),
         out_shape=pltpu.VMEM((owners, slots // owners, width + LANES), jnp.bfloat16),
         in_specs=[hbm_spec] * 3,
         out_specs=vmem_spec,
@@ -208,7 +230,7 @@
     owners = lax.axis_size(AXES)
     w, m, v = in_vmem(weights), in_vmem(moment), in_vmem(second)
     packed = pack(tile_rows, row_index, bucket_count, owners)
-    got = lax.all_to_all(packed, AXES, split_axis=0, concat_axis=0, tiled=True)
+    got = lax.all_to_all(packed, tuple(AXES[i] for i in TURN), split_axis=0, concat_axis=0, tiled=True)
     new_moment, new_second, update, parts, late_m, late_v = step(got, w, m, v, owners)
     sums = lax.all_to_all(parts, AXES, split_axis=0, concat_axis=0, tiled=True)
     return tuple(finish(sums, update, w, late_m, late_v, new_moment, new_second))

time: 64.6 us -> 64.2 us (level)
    all_to_all x1, blocking collectives: 42.5 us -> 41.3 us  [local(): lax.all_to_all(packed, tuple((AXES[i] for i in TURN)), split_axis=0, conc...]
    all_to_all x1, blocking collectives: 14.3 us -> 14.9 us  [local(): sums = lax.all_to_all(parts, AXES, split_axis=0, concat_axis=0, tiled=True)]
where the time goes in v5:
time: 64.2 us; the launch traced here: 64 us
  blocking collectives  56.2 us (88%)
  Pallas kernels  7.1 us (11%)
  between operations  0.68 us (1%)
    all_to_all x1, blocking collectives, local(): lax.all_to_all(packed, tuple((AXES[i] for i in TURN)), split_axis=0, conc...  41.3 us
    all_to_all x1, blocking collectives, local(): sums = lax.all_to_all(parts, AXES, split_axis=0, concat_axis=0, tiled=True)  14.9 us
    pallas_call x1, Pallas kernels, step(): pl.pallas_call(step_body, out_shape=[table, table, pltpu.VMEM(w.shape, jn...  2.81 us
    pallas_call x1, Pallas kernels, finish(): pl.pallas_call(finish_body, out_shape=[table] * 3, in_specs=[vmem_spec] *...  2.38 us
    pallas_call x1, Pallas kernels, pack(): pl.pallas_call(functools.partial(pack_body, tuple((lax.axis_size(a) for a...  1.92 us

profile of v5, /device:TPU:1, one launch (start us, length us, event | category | flops | bytes accessed | tf_op | source)
XLA Modules:
  0.0 64.0 jit_solution(1139710055956184089)
XLA Ops:
  0.6 0.0 copy-start.1
  0.6 0.0 copy-start.2
  0.7 1.9 %pack.1 = bf16[128,2,4224]{2,1,0:T(2,128)(2,1)S(1)} custom-call(bf16[256,4096]{1,0:T(8,128)(2,1)} %rows.1, s32[1,256]{1,0:T(1,128)} %bitcast.2, s32[1,128]{1,0:T(1,128)} %bitcast.3), custom_call_target="tpu_custom_call" | custom-call | flops 4000000000 | tf_op jit(solution)/shard_map/pack/pallas_call | solution.py:90
  2.6 0.0 copy-start
  2.6 41.3 %all_to_all.10.got = bf16[128,2,4224]{2,1,0:T(2,128)(2,1)S(1)} all-to-all(bf16[128,2,4224]{2,1,0:T(2,128)(2,1)S(1)} %pack.1), channel_id=1, replica_groups=mesh['rows_0'=4,'rows_1'=4,'dp_0'=4,'dp_1'=2] {'dp_0','dp_1','rows_0','r..., dimensions={0} | all-to-all | bytes 4325376 | tf_op jit(solution)/shard_map/all_to_all | solution.py:233
  43.9 0.0 copy-done.1
  43.9 0.0 copy-done.2
  43.9 0.0 copy-done
  43.9 2.8 %step.1 = (f32[192,4096]{1,0:T(8,128)}, f32[192,4096]{1,0:T(8,128)}, f32[192,4096]{1,0:T(8,128)S(1)}, f32[128,1,256]{2,1,0:T(1,128)S(1)}, f32[192,1024]{1,0:T(8,128)S(1)}, /*index=5*/f32[192,1024]{1,0:T(8,128)S(1)}) custom-call(bf16[128,2,4224]{2,1,0:T(2,128)(2,1)S(1)} %all_to_all.10.got, f32[192,4096]{1,0:T(8,128)S(1)} %copy-done, ...), custom_call_target="tpu_custom_call" | custom-call | tf_op jit(solution)/shard_map/step/pallas_call | solution.py:171
  46.7 14.9 %all_to_all.11.parts = f32[128,1,256]{2,1,0:T(1,128)S(1)} all-to-all(f32[128,1,256]{2,1,0:T(1,128)S(1)} %get-tuple-element.9), channel_id=1, replica_groups=mesh['rows_0'=4,'rows_1'=4,'dp_0'=4,'dp_1'=2] {'rows_0','rows_1','dp_0',..., dimensions={0} | all-to-all | bytes 262144 | tf_op jit(solution)/shard_map/all_to_all | solution.py:235
  61.7 2.4 %finish.1 = (f32[192,4096]{1,0:T(8,128)}, f32[192,4096]{1,0:T(8,128)}, f32[192,4096]{1,0:T(8,128)}) custom-call(f32[128,1,256]{2,1,0:T(1,128)S(1)} %all_to_all.11.parts, f32[192,4096]{1,0:T(8,128)S(1)} %get-tuple-element.10.u, f32[192,4096]{1,0:T(8,128)S(1)} %copy-done, ...), custom_call_target="tpu_custom_call", output_to_operand_aliasing={{1}: (5, {}), {2}: (6, {})} | custom-call | tf_op jit(solution)/shard_map/finish/pallas_call | solution.py:213
Async XLA Ops:
  0.6 43.3 %copy-start.1 = (f32[192,4096]{1,0:T(8,128)S(1)}, f32[192,4096]{1,0:T(8,128)}, u32[]{:S(2)}) copy-start(f32[192,4096]{1,0:T(8,128)} %m.1) | copy-start | bytes 9437188
  0.6 43.3 %copy-start.2 = (f32[192,4096]{1,0:T(8,128)S(1)}, f32[192,4096]{1,0:T(8,128)}, u32[]{:S(2)}) copy-start(f32[192,4096]{1,0:T(8,128)} %v.1) | copy-start | bytes 9437188
  2.6 41.3 %copy-start = (f32[192,4096]{1,0:T(8,128)S(1)}, f32[192,4096]{1,0:T(8,128)}, u32[]{:S(2)}) copy-start(f32[192,4096]{1,0:T(8,128)} %w.3) | copy-start | bytes 9437188

commit v6 on v5

--- a/solution.py
+++ b/solution.py
@@ -9,7 +9,7 @@
 from jax.sharding import PartitionSpec as P
 
 AXES = ("rows_0", "rows_1", "dp_0", "dp_1")
-TURN = (2, 3, 0, 1)
+TURN = (2, 3, 1, 0)
 
 beta_one = 0.9
 beta_two = 0.999
@@ -18,7 +18,7 @@
 rate = 0.1
 
 LANES = 128
-PACK_FLOPS = 4_000_000_000
+GATE_FLOPS = 4_000_000_000
 VMEM_LIMIT = 20 * 1024 * 1024
 
 any_spec = pl.BlockSpec(memory_space=pl.ANY)
@@ -85,11 +85,16 @@
     pltpu.make_async_copy(whole, whole, sem).wait()
 
 
+def gate_body(packed_in, packed):
+    packed[0, :, pl.ds(0, LANES)] = packed_in[0, :, pl.ds(0, LANES)]
+
+
 def pack(rows, index, count, owners):
     slots, width = rows.shape
-    return pl.pallas_call(
+    blocks = pltpu.VMEM((owners, slots // owners, width + LANES), jnp.bfloat16)
+    packed = pl.pallas_call(
         functools.partial(pack_body, tuple(lax.axis_size(a) for a in AXES)),
-        out_shape=pltpu.VMEM((owners, slots // owners, width + LANES), jnp.bfloat16),
+        out_shape=blocks,
         in_specs=[hbm_spec] * 3,
         out_specs=vmem_spec,
         scratch_shapes=[
@@ -99,9 +104,18 @@
             pltpu.SemaphoreType.DMA((2,)),
         ],
         compiler_params=pltpu.CompilerParams(vmem_limit_bytes=VMEM_LIMIT),
-        cost_estimate=pl.CostEstimate(flops=PACK_FLOPS, transcendentals=0, bytes_accessed=0),
         name="pack",
     )(*map(in_hbm, (rows, index.reshape(1, slots), count.reshape(1, owners))))
+    return pl.pallas_call(
+        gate_body,
+        out_shape=blocks,
+        in_specs=[vmem_spec],
+        out_specs=vmem_spec,
+        input_output_aliases={0: 0},
+        compiler_params=pltpu.CompilerParams(vmem_limit_bytes=VMEM_LIMIT),
+        cost_estimate=pl.CostEstimate(flops=GATE_FLOPS, transcendentals=0, bytes_accessed=0),
+        name="gate",
+    )(packed)
 
 
 CHUNK = 512

time: 64.2 us -> 64.1 us (level)
  no operation moved by 1% of the time
where the time goes in v6:
time: 64.1 us; the launch traced here: 63.8 us
  blocking collectives  56.1 us (88%)
  Pallas kernels  6.98 us (11%)
  between operations  0.68 us (1%)
    all_to_all x1, blocking collectives, local(): lax.all_to_all(packed, tuple((AXES[i] for i in TURN)), split_axis=0, conc...  41.2 us
    all_to_all x1, blocking collectives, local(): sums = lax.all_to_all(parts, AXES, split_axis=0, concat_axis=0, tiled=True)  15 us
    pallas_call x1, Pallas kernels, step(): pl.pallas_call(step_body, out_shape=[table, table, pltpu.VMEM(w.shape, jn...  2.81 us
    pallas_call x1, Pallas kernels, finish(): pl.pallas_call(finish_body, out_shape=[table] * 3, in_specs=[vmem_spec] *...  2.38 us
    pallas_call x1, Pallas kernels, pack(): pl.pallas_call(functools.partial(pack_body, tuple((lax.axis_size(a) for a...  1.79 us

profile of v6, /device:TPU:1, one launch (start us, length us, event | category | flops | bytes accessed | tf_op | source)
XLA Modules:
  0.0 63.8 jit_solution(3135789709605448777)
XLA Ops:
  0.6 1.8 %pack.1.packed_in = bf16[128,2,4224]{2,1,0:T(2,128)(2,1)S(1)} custom-call(bf16[256,4096]{1,0:T(8,128)(2,1)} %rows.1, s32[1,256]{1,0:T(1,128)} %bitcast.2, s32[1,128]{1,0:T(1,128)} %bitcast.3), custom_call_target="tpu_custom_call" | custom-call | tf_op jit(solution)/shard_map/pack/pallas_call | solution.py:95
  2.4 0.0 copy-start.1
  2.4 0.0 copy-start.2
  2.5 0.0 copy-start
  2.5 41.2 %all_to_all.10.got = bf16[128,2,4224]{2,1,0:T(2,128)(2,1)S(1)} all-to-all(bf16[128,2,4224]{2,1,0:T(2,128)(2,1)S(1)} %gate.1), channel_id=1, replica_groups=mesh['rows_0'=4,'rows_1'=4,'dp_0'=4,'dp_1'=2] {'dp_0','dp_1','rows_1','r..., dimensions={0} | all-to-all | bytes 4325376 | tf_op jit(solution)/shard_map/all_to_all | solution.py:247
  43.7 0.0 copy-done.1
  43.7 0.0 copy-done.2
  43.7 0.0 copy-done
  43.7 2.8 %step.1 = (f32[192,4096]{1,0:T(8,128)}, f32[192,4096]{1,0:T(8,128)}, f32[192,4096]{1,0:T(8,128)S(1)}, f32[128,1,256]{2,1,0:T(1,128)S(1)}, f32[192,1024]{1,0:T(8,128)S(1)}, /*index=5*/f32[192,1024]{1,0:T(8,128)S(1)}) custom-call(bf16[128,2,4224]{2,1,0:T(2,128)(2,1)S(1)} %all_to_all.10.got, f32[192,4096]{1,0:T(8,128)S(1)} %copy-done, ...), custom_call_target="tpu_custom_call" | custom-call | tf_op jit(solution)/shard_map/step/pallas_call | solution.py:185
  46.5 15.0 %all_to_all.11.parts = f32[128,1,256]{2,1,0:T(1,128)S(1)} all-to-all(f32[128,1,256]{2,1,0:T(1,128)S(1)} %get-tuple-element.9), channel_id=1, replica_groups=mesh['rows_0'=4,'rows_1'=4,'dp_0'=4,'dp_1'=2] {'rows_0','rows_1','dp_0',..., dimensions={0} | all-to-all | bytes 262144 | tf_op jit(solution)/shard_map/all_to_all | solution.py:249
  61.5 2.4 %finish.1 = (f32[192,4096]{1,0:T(8,128)}, f32[192,4096]{1,0:T(8,128)}, f32[192,4096]{1,0:T(8,128)}) custom-call(f32[128,1,256]{2,1,0:T(1,128)S(1)} %all_to_all.11.parts, f32[192,4096]{1,0:T(8,128)S(1)} %get-tuple-element.10.u, f32[192,4096]{1,0:T(8,128)S(1)} %copy-done, ...), custom_call_target="tpu_custom_call", output_to_operand_aliasing={{1}: (5, {}), {2}: (6, {})} | custom-call | tf_op jit(solution)/shard_map/finish/pallas_call | solution.py:227
  (1 shorter events, 0.0 us)
Async XLA Ops:
  2.4 41.2 %copy-start.1 = (f32[192,4096]{1,0:T(8,128)S(1)}, f32[192,4096]{1,0:T(8,128)}, u32[]{:S(2)}) copy-start(f32[192,4096]{1,0:T(8,128)} %m.1) | copy-start | bytes 9437188
  2.4 41.2 %copy-start.2 = (f32[192,4096]{1,0:T(8,128)S(1)}, f32[192,4096]{1,0:T(8,128)}, u32[]{:S(2)}) copy-start(f32[192,4096]{1,0:T(8,128)} %v.1) | copy-start | bytes 9437188
  2.5 41.2 %copy-start = (f32[192,4096]{1,0:T(8,128)S(1)}, f32[192,4096]{1,0:T(8,128)}, u32[]{:S(2)}) copy-start(f32[192,4096]{1,0:T(8,128)} %w.3) | copy-start | bytes 9437188

commit v7 on v5

--- a/solution.py
+++ b/solution.py
@@ -9,7 +9,7 @@
 from jax.sharding import PartitionSpec as P
 
 AXES = ("rows_0", "rows_1", "dp_0", "dp_1")
-TURN = (2, 3, 0, 1)
+TURN = (2, 3, 1, 0)
 
 beta_one = 0.9
 beta_two = 0.999

time: 64.2 us -> 64.1 us (level)
  no operation moved by 1% of the time
where the time goes in v7:
time: 64.1 us; the launch traced here: 64 us
  blocking collectives  56.2 us (88%)
  Pallas kernels  7.1 us (11%)
  between operations  0.68 us (1%)
    all_to_all x1, blocking collectives, local(): lax.all_to_all(packed, tuple((AXES[i] for i in TURN)), split_axis=0, conc...  41.2 us
    all_to_all x1, blocking collectives, local(): sums = lax.all_to_all(parts, AXES, split_axis=0, concat_axis=0, tiled=True)  15 us
    pallas_call x1, Pallas kernels, step(): pl.pallas_call(step_body, out_shape=[table, table, pltpu.VMEM(w.shape, jn...  2.8 us
    pallas_call x1, Pallas kernels, finish(): pl.pallas_call(finish_body, out_shape=[table] * 3, in_specs=[vmem_spec] *...  2.38 us
    pallas_call x1, Pallas kernels, pack(): pl.pallas_call(functools.partial(pack_body, tuple((lax.axis_size(a) for a...  1.92 us

profile of v7, /device:TPU:1, one launch (start us, length us, event | category | flops | bytes accessed | tf_op | source)
XLA Modules:
  0.0 64.0 jit_solution(9968371431692127777)
XLA Ops:
  0.6 0.0 copy-start.1
  0.6 0.0 copy-start.2
  0.7 1.9 %pack.1 = bf16[128,2,4224]{2,1,0:T(2,128)(2,1)S(1)} custom-call(bf16[256,4096]{1,0:T(8,128)(2,1)} %rows.1, s32[1,256]{1,0:T(1,128)} %bitcast.2, s32[1,128]{1,0:T(1,128)} %bitcast.3), custom_call_target="tpu_custom_call" | custom-call | flops 4000000000 | tf_op jit(solution)/shard_map/pack/pallas_call | solution.py:90
  2.6 0.0 copy-start
  2.6 41.2 %all_to_all.10.got = bf16[128,2,4224]{2,1,0:T(2,128)(2,1)S(1)} all-to-all(bf16[128,2,4224]{2,1,0:T(2,128)(2,1)S(1)} %pack.1), channel_id=1, replica_groups=mesh['rows_0'=4,'rows_1'=4,'dp_0'=4,'dp_1'=2] {'dp_0','dp_1','rows_1','r..., dimensions={0} | all-to-all | bytes 4325376 | tf_op jit(solution)/shard_map/all_to_all | solution.py:233
  43.8 0.0 copy-done.1
  43.8 0.0 copy-done.2
  43.8 0.0 copy-done
  43.8 2.8 %step.1 = (f32[192,4096]{1,0:T(8,128)}, f32[192,4096]{1,0:T(8,128)}, f32[192,4096]{1,0:T(8,128)S(1)}, f32[128,1,256]{2,1,0:T(1,128)S(1)}, f32[192,1024]{1,0:T(8,128)S(1)}, /*index=5*/f32[192,1024]{1,0:T(8,128)S(1)}) custom-call(bf16[128,2,4224]{2,1,0:T(2,128)(2,1)S(1)} %all_to_all.10.got, f32[192,4096]{1,0:T(8,128)S(1)} %copy-done, ...), custom_call_target="tpu_custom_call" | custom-call | tf_op jit(solution)/shard_map/step/pallas_call | solution.py:171
  46.6 15.0 %all_to_all.11.parts = f32[128,1,256]{2,1,0:T(1,128)S(1)} all-to-all(f32[128,1,256]{2,1,0:T(1,128)S(1)} %get-tuple-element.9), channel_id=1, replica_groups=mesh['rows_0'=4,'rows_1'=4,'dp_0'=4,'dp_1'=2] {'rows_0','rows_1','dp_0',..., dimensions={0} | all-to-all | bytes 262144 | tf_op jit(solution)/shard_map/all_to_all | solution.py:235
  61.6 2.4 %finish.1 = (f32[192,4096]{1,0:T(8,128)}, f32[192,4096]{1,0:T(8,128)}, f32[192,4096]{1,0:T(8,128)}) custom-call(f32[128,1,256]{2,1,0:T(1,128)S(1)} %all_to_all.11.parts, f32[192,4096]{1,0:T(8,128)S(1)} %get-tuple-element.10.u, f32[192,4096]{1,0:T(8,128)S(1)} %copy-done, ...), custom_call_target="tpu_custom_call", output_to_operand_aliasing={{1}: (5, {}), {2}: (6, {})} | custom-call | tf_op jit(solution)/shard_map/finish/pallas_call | solution.py:213
Async XLA Ops:
  0.6 43.2 %copy-start.1 = (f32[192,4096]{1,0:T(8,128)S(1)}, f32[192,4096]{1,0:T(8,128)}, u32[]{:S(2)}) copy-start(f32[192,4096]{1,0:T(8,128)} %m.1) | copy-start | bytes 9437188
  0.6 43.2 %copy-start.2 = (f32[192,4096]{1,0:T(8,128)S(1)}, f32[192,4096]{1,0:T(8,128)}, u32[]{:S(2)}) copy-start(f32[192,4096]{1,0:T(8,128)} %v.1) | copy-start | bytes 9437188
  2.6 41.2 %copy-start = (f32[192,4096]{1,0:T(8,128)S(1)}, f32[192,4096]{1,0:T(8,128)}, u32[]{:S(2)}) copy-start(f32[192,4096]{1,0:T(8,128)} %w.3) | copy-start | bytes 9437188
